TPU v7x, 32 devices: a whole 2x2x4 slice. The times are simulated.
32 devices in a mesh: row: 8 (over z, x), col: 4 (over y, core).
Axes of the slice: x: 2, y: 2, z: 4, core: 2. Of those that a mesh axis runs over, the one named last changes fastest.
Arguments:
- hidden_in: bfloat16 [32, 512, 1024], P('row', 'col'), may hold values from -6 to 6
- first_values: bfloat16 [32, 1024, 512], P('row', 'col'), may hold values from -6 to 6
- lengths: int32 [32, 4], P('row'), may hold values from 1 to 256, 512 in all within a row
- places: int32 [32, 512], P('row'), may hold values from 0 to 511, each once within a row
- gain_attn: float32 [1024], replicated, may hold values from 0.1 to 1.9
- gain_ffn: float32 [1024], replicated, may hold values from 0.1 to 1.9
- w_query: bfloat16 [1024, 1024], P('row', 'col'), may hold values from -0.1875 to 0.1875
- w_key: bfloat16 [1024, 1024], P('row', 'col'), may hold values from -0.1875 to 0.1875
- w_value: bfloat16 [1024, 1024], P('row', 'col'), may hold values from -0.1875 to 0.1875
- w_out: bfloat16 [1024, 1024], P('col', 'row'), may hold values from -3 to 3
- w_gate: bfloat16 [1024, 2816], P('row', 'col'), may hold values from -0.1875 to 0.1875
- w_up: bfloat16 [1024, 2816], P('row', 'col'), may hold values from -0.1875 to 0.1875
- w_down: bfloat16 [2816, 1024], P('col', 'row'), may hold values from -0.109375 to 0.109375
- out_grad: bfloat16 [32, 512, 1024], P('row', 'col'), may hold values from -6 to 6
Outputs:
- layer_out: bfloat16 [32, 512, 1024], P('row', 'col')
- grad_hidden: float32 [32, 512, 1024], P('row', 'col')
- grad_first_values: float32 [32, 1024, 512], P('row', 'col')
- grad_gain_attn: float32 [1024], replicated
- grad_gain_ffn: float32 [1024], replicated
- grad_w_query: float32 [1024, 1024], P('row', 'col')
- grad_w_key: float32 [1024, 1024], P('row', 'col')
- grad_w_value: float32 [1024, 1024], P('row', 'col')
- grad_w_out: float32 [1024, 1024], P('col', 'row')
- grad_w_gate: float32 [1024, 2816], P('row', 'col')
- grad_w_up: float32 [1024, 2816], P('row', 'col')
- grad_w_down: float32 [2816, 1024], P('col', 'row')
Inputs may be any that keep to these rules, and one draw needn't show every extreme that they name: Each row of lengths sums to 512; the largest length in the draw is 256. Each row of places holds every number of 0 to 511 once.
All inputs are finite; a program needn't handle non-finite values.
Results may differ from a plain program's by a relative error of at most 0.015.
Values may be sent and summed in bfloat16 or wider, within the bound.
A program may use at most 192 MiB of HBM per device.

v0:
```python
import jax
import jax.numpy as jnp
from jax import lax
from jax.sharding import PartitionSpec as P

D = 1024
HEAD_DIM = 64
TOK_MB = 512
MICRO = 4
EPSILON = 1e-06
MASKED = -1e30


def product(left, right):
    return jnp.dot(left, right, preferred_element_type=jnp.float32)


def product_left(left, right):
    return lax.dot_general(
        left, right, (((0,), (0,)), ((), ())), preferred_element_type=jnp.float32
    )


def product_right(left, right):
    return lax.dot_general(
        left, right, (((1,), (1,)), ((), ())), preferred_element_type=jnp.float32
    )


def token_places(lengths_row, count):
    ends_at = jnp.cumsum(lengths_row)
    index_row = jnp.arange(count, dtype=jnp.int32)
    segment_id = jnp.sum((index_row[:, None] >= ends_at[None, :]).astype(jnp.int32), axis=1)
    starts_at = ends_at - lengths_row
    one_hot = segment_id[:, None] == jnp.arange(lengths_row.shape[0], dtype=jnp.int32)[None, :]
    position = index_row - jnp.sum(jnp.where(one_hot, starts_at[None, :], 0), axis=1)
    return (segment_id, position)


def rotary_tables(position):
    half_dim = HEAD_DIM // 2
    freq_index = jnp.arange(half_dim, dtype=jnp.float32)
    inverse = 10000.0 ** (-freq_index / half_dim)
    angles = position.astype(jnp.float32)[:, None] * inverse[None, :]
    return (jnp.cos(angles)[:, None, :], jnp.sin(angles)[:, None, :])


def rotate(field, cosine, sine):
    half_dim = field.shape[-1] // 2
    first_half, second_half = (field[..., :half_dim], field[..., half_dim:])
    return jnp.concatenate(
        [first_half * cosine - second_half * sine, second_half * cosine + first_half * sine],
        axis=-1,
    )


def rotate_back(field, cosine, sine):
    half_dim = field.shape[-1] // 2
    first_half, second_half = (field[..., :half_dim], field[..., half_dim:])
    return jnp.concatenate(
        [first_half * cosine + second_half * sine, second_half * cosine - first_half * sine],
        axis=-1,
    )


def spread_tokens(values):
    return lax.all_gather(values, "col", axis=0, tiled=True)


def reduce_tokens(values):
    return lax.psum_scatter(values, "col", scatter_dimension=0, tiled=True)


def body(
    hidden_in,
    first_values,
    lengths,
    places,
    gain_attn,
    gain_ffn,
    w_query,
    w_key,
    w_value,
    w_out,
    w_gate,
    w_up,
    w_down,
    out_grad,
):
    width_col = w_query.shape[1]
    heads_col = width_col // HEAD_DIM
    block_rows = min(512, TOK_MB)
    block_count = TOK_MB // block_rows
    local_rows = hidden_in.shape[1]
    row_start = lax.axis_index("col") * local_rows
    score_scale = HEAD_DIM ** (-0.5)
    tiles = (w_query, w_key, w_value, w_out, w_gate, w_up, w_down)

    def own_rows(values):
        return lax.dynamic_slice_in_dim(values, row_start, local_rows)

    hidden_width = w_gate.shape[1]
    full_shapes = (
        (D, width_col),
        (D, width_col),
        (D, width_col),
        (width_col, D),
        (D, hidden_width),
        (D, hidden_width),
        (hidden_width, D),
    )
    grads_full = tuple((jnp.zeros(shape_item, jnp.float32) for shape_item in full_shapes))
    grads_tile = tuple((jnp.zeros(tile_item.shape, jnp.float32) for tile_item in tiles))
    gain_sum_one = jnp.zeros((D,), jnp.float32)
    gain_sum_two = jnp.zeros((D,), jnp.float32)
    out_pieces, input_pieces, value_pieces = ([], [], [])
    for micro_step in range(MICRO):
        gathered = (
            lax.all_gather(tiles[0], "row", axis=0, tiled=True),
            lax.all_gather(tiles[1], "row", axis=0, tiled=True),
            lax.all_gather(tiles[2], "row", axis=0, tiled=True),
            lax.all_gather(tiles[3], "row", axis=1, tiled=True),
            lax.all_gather(tiles[4], "row", axis=0, tiled=True),
            lax.all_gather(tiles[5], "row", axis=0, tiled=True),
            lax.all_gather(tiles[6], "row", axis=1, tiled=True),
        )
        wq_all, wk_all, wv_all, wo_all, wg_all, wu_all, wd_all = gathered
        places_mb = places[micro_step]
        packed_order = (
            jnp.zeros((TOK_MB,), jnp.int32).at[places_mb].set(jnp.arange(TOK_MB, dtype=jnp.int32))
        )
        stored_hidden, stored_grad = (
            lax.all_gather(hidden_in[micro_step], "col", axis=0, tiled=True),
            lax.all_gather(out_grad[micro_step], "col", axis=0, tiled=True),
        )
        hidden_full = jnp.take(stored_hidden, packed_order, axis=0).astype(jnp.float32)
        grad_full_rows = jnp.take(stored_grad, packed_order, axis=0)
        first_mb = jnp.take(jnp.transpose(first_values[micro_step]), packed_order, axis=0).astype(
            jnp.float32
        )
        hidden_mb = own_rows(hidden_full)
        grad_mb = own_rows(grad_full_rows)
        segment_id, position = token_places(lengths[micro_step], TOK_MB)
        cosine, sine = rotary_tables(position)
        token_index = jnp.arange(TOK_MB, dtype=jnp.int32)
        scale_full = lax.rsqrt(jnp.mean(hidden_full * hidden_full, axis=1, keepdims=True) + EPSILON)
        scale_one = own_rows(scale_full)
        normed_one = (hidden_full * scale_full * gain_attn).astype(jnp.bfloat16)
        query_raw = product(normed_one, wq_all).reshape(TOK_MB, heads_col, HEAD_DIM)
        key_raw = product(normed_one, wk_all).reshape(TOK_MB, heads_col, HEAD_DIM)
        queries = rotate(query_raw, cosine, sine).astype(jnp.bfloat16)
        keys = rotate(key_raw, cosine, sine).astype(jnp.bfloat16)
        values = (
            (0.5 * product(normed_one, wv_all) + 0.5 * first_mb)
            .astype(jnp.bfloat16)
            .reshape(TOK_MB, heads_col, HEAD_DIM)
        )

        def block_scores(start_row):
            query_index = start_row + jnp.arange(block_rows, dtype=jnp.int32)
            allowed = (segment_id[:, None] == segment_id[None, :]) & (
                query_index[:, None] >= token_index[None, :]
            )
            raw_scores = (
                jnp.einsum("qhd,khd->hqk", queries, keys, preferred_element_type=jnp.float32)
                * score_scale
            )
            return (queries, jnp.where(allowed[None], raw_scores, MASKED))

        def attend(block_index):
            query_block, scores = block_scores(block_index * block_rows)
            row_top = jnp.max(scores, axis=-1, keepdims=True)
            log_total = row_top + jnp.log(
                jnp.sum(jnp.exp(scores - row_top), axis=-1, keepdims=True)
            )
            probs = jnp.exp(scores - log_total).astype(jnp.bfloat16)
            mixed = jnp.einsum("hqk,khd->qhd", probs, values, preferred_element_type=jnp.float32)
            return (mixed.astype(jnp.bfloat16), log_total[..., 0])

        attended, log_totals = lax.map(attend, jnp.arange(block_count, dtype=jnp.int32))
        attended = attended.reshape(TOK_MB, width_col)
        mid_mb = hidden_mb + reduce_tokens(product(attended, wo_all))
        scale_two = lax.rsqrt(jnp.mean(mid_mb * mid_mb, axis=1, keepdims=True) + EPSILON)
        normed_two = spread_tokens((mid_mb * scale_two * gain_ffn).astype(jnp.bfloat16))
        gate_raw = product(normed_two, wg_all)
        up_raw = product(normed_two, wu_all)
        sigmoid_gate = jax.nn.sigmoid(gate_raw)
        silu_gate = gate_raw * sigmoid_gate
        hidden_act = (silu_gate * up_raw).astype(jnp.bfloat16)
        packed_out = (mid_mb + reduce_tokens(product(hidden_act, wd_all))).astype(jnp.bfloat16)
        grad_down = product_left(hidden_act, grad_full_rows)
        d_hidden = product_right(grad_full_rows, wd_all)
        d_gate = (
            d_hidden * up_raw * sigmoid_gate * (1.0 + gate_raw * (1.0 - sigmoid_gate))
        ).astype(jnp.bfloat16)
        d_up = (d_hidden * silu_gate).astype(jnp.bfloat16)
        grad_gate = product_left(normed_two, d_gate)
        grad_up = product_left(normed_two, d_up)
        d_normed_two = reduce_tokens(product_right(d_gate, wg_all) + product_right(d_up, wu_all))
        gain_sum_two = gain_sum_two + jnp.sum(d_normed_two * mid_mb * scale_two, axis=0)
        scaled_two = d_normed_two * gain_ffn
        stat_two = jnp.sum(scaled_two * mid_mb, axis=1, keepdims=True)
        d_mid = (
            grad_mb.astype(jnp.float32)
            + scale_two * scaled_two
            - mid_mb * (scale_two * scale_two * scale_two * stat_two / D)
        )
        d_branch = spread_tokens(d_mid.astype(jnp.bfloat16))
        grad_out = product_left(attended, d_branch)
        d_attended = (
            product_right(d_branch, wo_all)
            .astype(jnp.bfloat16)
            .reshape(TOK_MB, heads_col, HEAD_DIM)
        )

        def attend_back(carry, block_index):
            key_acc, value_acc = carry
            start_row = block_index * block_rows
            query_block, scores = block_scores(start_row)
            log_block = log_totals[block_index]
            probs = jnp.exp(scores - log_block[..., None])
            d_probs = jnp.einsum(
                "qhd,khd->hqk", d_attended, values, preferred_element_type=jnp.float32
            )
            inner_sum = jnp.sum(probs * d_probs, axis=-1, keepdims=True)
            d_scores = (probs * (d_probs - inner_sum)).astype(jnp.bfloat16)
            d_query = (
                jnp.einsum("hqk,khd->qhd", d_scores, keys, preferred_element_type=jnp.float32)
                * score_scale
            )
            key_acc = (
                key_acc
                + jnp.einsum(
                    "hqk,qhd->khd", d_scores, query_block, preferred_element_type=jnp.float32
                )
                * score_scale
            )
            value_acc = value_acc + jnp.einsum(
                "hqk,qhd->khd",
                probs.astype(jnp.bfloat16),
                d_attended,
                preferred_element_type=jnp.float32,
            )
            return ((key_acc, value_acc), d_query)

        empty_heads = jnp.zeros((TOK_MB, heads_col, HEAD_DIM), jnp.float32)
        (key_grads, value_grads), query_grads = lax.scan(
            attend_back, (empty_heads, empty_heads), jnp.arange(block_count, dtype=jnp.int32)
        )
        d_values = value_grads.astype(jnp.bfloat16).reshape(TOK_MB, width_col)
        half_values = 0.5 * d_values.astype(jnp.float32)
        value_pieces.append(jnp.transpose(jnp.take(half_values, places_mb, axis=0)))
        d_value_proj = half_values.astype(jnp.bfloat16)
        d_query_raw = (
            rotate_back(query_grads.reshape(TOK_MB, heads_col, HEAD_DIM), cosine, sine)
            .astype(jnp.bfloat16)
            .reshape(TOK_MB, width_col)
        )
        d_key_raw = (
            rotate_back(key_grads, cosine, sine).astype(jnp.bfloat16).reshape(TOK_MB, width_col)
        )
        grad_query = product_left(normed_one, d_query_raw)
        grad_key = product_left(normed_one, d_key_raw)
        grad_value = product_left(normed_one, d_value_proj)
        d_normed_one = reduce_tokens(
            product_right(d_query_raw, wq_all)
            + product_right(d_key_raw, wk_all)
            + product_right(d_value_proj, wv_all)
        )
        gain_sum_one = gain_sum_one + jnp.sum(d_normed_one * hidden_mb * scale_one, axis=0)
        scaled_one = d_normed_one * gain_attn
        stat_one = jnp.sum(scaled_one * hidden_mb, axis=1, keepdims=True)
        packed_input = (
            d_mid
            + scale_one * scaled_one
            - hidden_mb * (scale_one * scale_one * scale_one * stat_one / D)
        )
        out_whole, input_whole = (
            lax.all_gather(
                packed_out.astype(jnp.float32).astype(jnp.bfloat16), "col", axis=0, tiled=True
            ).astype(jnp.float32),
            lax.all_gather(packed_input.astype(jnp.bfloat16), "col", axis=0, tiled=True).astype(
                packed_input.dtype
            ),
        )
        stored_places = lax.dynamic_slice_in_dim(places_mb, row_start, local_rows)
        out_pieces.append(jnp.take(out_whole, stored_places, axis=0).astype(jnp.bfloat16))
        input_pieces.append(jnp.take(input_whole, stored_places, axis=0))
        new_grads = (grad_query, grad_key, grad_value, grad_out, grad_gate, grad_up, grad_down)
        grads_full = tuple((earlier + later for earlier, later in zip(grads_full, new_grads)))
    grads_tile = (
        lax.psum_scatter(
            grads_full[0].astype(jnp.bfloat16), "row", scatter_dimension=0, tiled=True
        ).astype(jnp.float32),
        lax.psum_scatter(
            grads_full[1].astype(jnp.bfloat16), "row", scatter_dimension=0, tiled=True
        ).astype(jnp.float32),
        lax.psum_scatter(
            grads_full[2].astype(jnp.bfloat16), "row", scatter_dimension=0, tiled=True
        ).astype(jnp.float32),
        lax.psum_scatter(
            grads_full[3].astype(jnp.bfloat16), "row", scatter_dimension=1, tiled=True
        ).astype(jnp.float32),
        lax.psum_scatter(
            grads_full[4].astype(jnp.bfloat16), "row", scatter_dimension=0, tiled=True
        ).astype(jnp.float32),
        lax.psum_scatter(
            grads_full[5].astype(jnp.bfloat16), "row", scatter_dimension=0, tiled=True
        ).astype(jnp.float32),
        lax.psum_scatter(
            grads_full[6].astype(jnp.bfloat16), "row", scatter_dimension=1, tiled=True
        ).astype(jnp.float32),
    )
    gain_grad_one, gain_grad_two = lax.psum((gain_sum_one, gain_sum_two), ("row", "col"))
    return (
        jnp.stack(out_pieces, axis=0),
        jnp.stack(input_pieces, axis=0),
        jnp.stack(value_pieces, axis=0),
        gain_grad_one,
        gain_grad_two,
        grads_tile[0],
        grads_tile[1],
        grads_tile[2],
        grads_tile[3],
        grads_tile[4],
        grads_tile[5],
        grads_tile[6],
    )


def solution(mesh):
    return jax.shard_map(
        body,
        mesh=mesh,
        in_specs=(
            P("row", "col", None),
            P("row", "col", None),
            P("row", None),
            P("row", None),
            P(),
            P(),
            P("row", "col"),
            P("row", "col"),
            P("row", "col"),
            P("col", "row"),
            P("row", "col"),
            P("row", "col"),
            P("col", "row"),
            P("row", "col", None),
        ),
        out_specs=(
            P("row", "col", None),
            P("row", "col", None),
            P("row", "col", None),
            P(),
            P(),
            P("row", "col"),
            P("row", "col"),
            P("row", "col"),
            P("col", "row"),
            P("row", "col"),
            P("row", "col"),
            P("col", "row"),
        ),
        check_vma=False,
    )
```

profile of v0, /device:TPU:0, one launch (start us, length us, event | category | flops | bytes accessed | tf_op | source)
XLA Modules:
  0.0 1710.5 jit_solution(1301464961985849624)
XLA Ops:
  24.7 33.2 %all_gather.116 = bf16[1024,256]{1,0:T(8,128)(2,1)S(1)} all-gather(bf16[128,256]{1,0:T(8,128)(2,1)S(1)} %copy-done.200), channel_id=1, replica_groups=mesh['row'=8,'col'=4] {'row'}, dimensions={0}, use_global_device_ids=true | all-gather | bytes 589824 | tf_op jit(solution)/shard_map/all_gather | solution.py:119
  59.1 31.5 %all_gather.117 = bf16[1024,256]{1,0:T(8,128)(2,1)S(1)} all-gather(bf16[128,256]{1,0:T(8,128)(2,1)S(1)} %copy-done.201), channel_id=1, replica_groups=mesh['row'=8,'col'=4] {'row'}, dimensions={0}, use_global_device_ids=true | all-gather | bytes 589824 | tf_op jit(solution)/shard_map/all_gather | solution.py:120
  90.7 33.4 %all_gather.115 = bf16[1024,256]{1,0:T(8,128)(2,1)} all-gather(bf16[128,256]{1,0:T(8,128)(2,1)S(1)} %copy-done.202), channel_id=1, replica_groups=mesh['row'=8,'col'=4] {'row'}, dimensions={0}, use_global_device_ids=true | all-gather | bytes 589824 | tf_op jit(solution)/shard_map/all_gather | solution.py:121
  125.0 28.3 %all_gather.118 = bf16[256,1024]{1,0:T(8,128)(2,1)} all-gather(bf16[256,128]{1,0:T(8,128)(2,1)S(1)} %copy-done.203), channel_id=1, replica_groups=mesh['row'=8,'col'=4] {'row'}, dimensions={1}, use_global_device_ids=true | all-gather | bytes 589824 | tf_op jit(solution)/shard_map/all_gather | solution.py:122
  158.0 4.1 gather_fusion
  163.1 4.1 gather_fusion.3
  168.3 4.1 gather_fusion.6
  174.1 4.1 gather_fusion.9
  179.3 4.1 multiply_convert_fusion.7
  192.5 4.8 gather_fusion.12
  197.4 3.8 broadcast_select_fusion.3
  201.2 21.0 %reduce-scatter.32.cloned.1.call-done = f32[128,1024]{1,0:T(8,128)} async-done(((f32[512,1024]{1,0:T(8,128)}), f32[128,1024]{1,0:T(8,128)}) %reduce-scatter.32.cloned.1.call-update) | async-done | bytes 524304 | tf_op jit(solution)/shard_map/reduce_scatter | solution.py:71
  226.6 40.7 %all-gather.38.cloned.1.call-done = bf16[1024,704]{0,1:T(8,128)(2,1)} async-done(((bf16[128,704]{0,1:T(8,128)(2,1)}), bf16[1024,704]{0,1:T(8,128)(2,1)}) %all-gather.38.cloned.1.call-update) | async-done | bytes 1441808 | tf_op jit(solution)/shard_map/all_gather | solution.py:123
  267.3 17.1 all-gather.36.cloned.1.call-done
  284.3 3.7 fusion.120
  288.1 41.3 %all-gather.40.cloned.1.call-done = bf16[1024,704]{0,1:T(8,128)(2,1)} async-done(((bf16[128,704]{0,1:T(8,128)(2,1)}), bf16[1024,704]{0,1:T(8,128)(2,1)}) %all-gather.40.cloned.1.call-update) | async-done | bytes 1441808 | tf_op jit(solution)/shard_map/all_gather | solution.py:124
  329.4 3.7 fusion.121
  333.1 39.4 %all-gather.42.cloned.1.call-done = bf16[704,1024]{1,0:T(8,128)(2,1)} async-done(((bf16[704,128]{1,0:T(8,128)(2,1)}), bf16[704,1024]{1,0:T(8,128)(2,1)}) %all-gather.42.cloned.1.call-update) | async-done | bytes 1441808 | tf_op jit(solution)/shard_map/all_gather | solution.py:125
  372.5 5.0 multiply_convert_fusion.14
  381.8 29.5 %reduce-scatter.48.cloned.1.call-done = f32[128,1024]{1,0:T(8,128)} async-done(((f32[512,1024]{1,0:T(8,128)}), f32[128,1024]{1,0:T(8,128)}) %reduce-scatter.48.cloned.1.call-update) | async-done | bytes 524304 | tf_op jit(solution)/shard_map/reduce_scatter | solution.py:71
  459.7 3.9 multiply_reduce_fusion.3
  473.1 3.7 fusion.122
  478.4 4.8 gather_fusion.18
  483.3 4.8 gather_fusion.16
  488.1 4.9 gather_fusion.14
  493.1 3.3 broadcast_select_fusion.2
  499.7 20.8 %reduce-scatter.36.cloned.1.call-done = f32[128,1024]{1,0:T(8,128)} async-done(((f32[512,1024]{1,0:T(8,128)}), f32[128,1024]{1,0:T(8,128)}) %reduce-scatter.36.cloned.1.call-update) | async-done | bytes 524304 | tf_op jit(solution)/shard_map/reduce_scatter | solution.py:71
  522.4 32.3 %reduce-scatter.40.cloned.1.call-done = f32[128,1024]{1,0:T(8,128)} async-done(((f32[512,1024]{1,0:T(8,128)}), f32[128,1024]{1,0:T(8,128)}) %reduce-scatter.40.cloned.1.call-update) | async-done | bytes 524304 | tf_op jit(solution)/shard_map/reduce_scatter | solution.py:71
  557.3 30.9 %reduce-scatter.44.cloned.1.call-done = f32[128,1024]{1,0:T(8,128)} async-done(((f32[512,1024]{1,0:T(8,128)}), f32[128,1024]{1,0:T(8,128)}) %reduce-scatter.44.cloned.1.call-update) | async-done | bytes 524304 | tf_op jit(solution)/shard_map/reduce_scatter | solution.py:71
  590.7 31.3 %reduce-scatter.50.cloned.1.call-done = f32[128,1024]{1,0:T(8,128)} async-done(((f32[512,1024]{1,0:T(8,128)}), f32[128,1024]{1,0:T(8,128)}) %reduce-scatter.50.cloned.1.call-update) | async-done | bytes 524304 | tf_op jit(solution)/shard_map/reduce_scatter | solution.py:71
  625.2 30.4 %reduce-scatter.34.cloned.1.call-done = f32[128,1024]{1,0:T(8,128)} async-done(((f32[512,1024]{1,0:T(8,128)}), f32[128,1024]{1,0:T(8,128)}) %reduce-scatter.34.cloned.1.call-update) | async-done | bytes 524304 | tf_op jit(solution)/shard_map/reduce_scatter | solution.py:71
  658.9 16.8 all-gather.46.cloned.1.call-done
  686.1 31.3 %reduce-scatter.52.cloned.1.call-done = f32[128,1024]{1,0:T(8,128)} async-done(((f32[512,1024]{1,0:T(8,128)}), f32[128,1024]{1,0:T(8,128)}) %reduce-scatter.52.cloned.1.call-update) | async-done | bytes 524304 | tf_op jit(solution)/shard_map/reduce_scatter | solution.py:71
  724.3 15.1 all-gather.62.cloned.1.call-done
  741.1 3.9 multiply_reduce_fusion.2
  753.4 4.0 fusion.128
  768.1 7.7 all-gather.50.cloned.1.call-done
  787.5 22.5 %reduce-scatter.54.cloned.1.call-done = f32[128,1024]{1,0:T(8,128)} async-done(((f32[512,1024]{1,0:T(8,128)}), f32[128,1024]{1,0:T(8,128)}) %reduce-scatter.54.cloned.1.call-update) | async-done | bytes 524304 | tf_op jit(solution)/shard_map/reduce_scatter | solution.py:71
  813.2 30.4 %reduce-scatter.38.cloned.1.call-done = f32[128,1024]{1,0:T(8,128)} async-done(((f32[512,1024]{1,0:T(8,128)}), f32[128,1024]{1,0:T(8,128)}) %reduce-scatter.38.cloned.1.call-update) | async-done | bytes 524304 | tf_op jit(solution)/shard_map/reduce_scatter | solution.py:71
  843.5 33.7 %reduce-scatter.60.cloned.1.call-done = f32[128,1024]{1,0:T(8,128)} async-done(((f32[512,1024]{1,0:T(8,128)}), f32[128,1024]{1,0:T(8,128)}) %reduce-scatter.60.cloned.1.call-update) | async-done | bytes 524304 | tf_op jit(solution)/shard_map/reduce_scatter | solution.py:71
  877.3 33.7 %reduce-scatter.56.cloned.1.call-done = f32[128,1024]{1,0:T(8,128)} async-done(((f32[512,1024]{1,0:T(8,128)}), f32[128,1024]{1,0:T(8,128)}) %reduce-scatter.56.cloned.1.call-update) | async-done | bytes 524304 | tf_op jit(solution)/shard_map/reduce_scatter | solution.py:71
  911.0 4.1 subtract_convert_fusion.2
  918.3 16.1 all-gather.66.cloned.1.call-done
  936.1 3.9 multiply_reduce_fusion.1
  949.6 3.7 fusion.134
  955.5 3.9 multiply_reduce_fusion
  967.8 3.7 fusion.140
  1016.7 3.9 reduce-scatter.42.cloned.1.call-done
  1020.5 34.3 %reduce-scatter.62.cloned.1.call-done = f32[128,1024]{1,0:T(8,128)} async-done(((f32[512,1024]{1,0:T(8,128)}), f32[128,1024]{1,0:T(8,128)}) %reduce-scatter.62.cloned.1.call-update) | async-done | bytes 524304 | tf_op jit(solution)/shard_map/reduce_scatter | solution.py:71
  1057.9 30.7 %reduce-scatter.46.cloned.1.call-done = f32[128,1024]{1,0:T(8,128)} async-done(((f32[512,1024]{1,0:T(8,128)}), f32[128,1024]{1,0:T(8,128)}) %reduce-scatter.46.cloned.1.call-update) | async-done | bytes 524304 | tf_op jit(solution)/shard_map/reduce_scatter | solution.py:71
  1095.1 12.2 all-gather.60.cloned.1.call-done
  1109.6 16.4 all-gather.44.cloned.1.call-done
  1129.5 65.5 %reduce-scatter.72.cloned.1.call-done = bf16[128,704]{1,0:T(8,128)(2,1)} async-done(((bf16[1024,704]{1,0:T(8,128)(2,1)}), bf16[128,704]{1,0:T(8,128)(2,1)}) %reduce-scatter.72.cloned.1.call-update) | async-done | bytes 180240
  1196.9 65.9 %reduce-scatter.74.cloned.1.call-done = bf16[128,704]{1,0:T(8,128)(2,1)} async-done(((bf16[1024,704]{1,0:T(8,128)(2,1)}), bf16[128,704]{1,0:T(8,128)(2,1)}) %reduce-scatter.74.cloned.1.call-update) | async-done | bytes 180240
  1264.6 65.9 %reduce-scatter.76.cloned.1.call-done = bf16[128,704]{1,0:T(8,128)(2,1)} async-done(((bf16[1024,704]{1,0:T(8,128)(2,1)}), bf16[128,704]{1,0:T(8,128)(2,1)}) %reduce-scatter.76.cloned.1.call-update) | async-done | bytes 180240
  1343.1 4.6 all-gather.64.cloned.1.call-done
  1350.0 16.0 all-gather.48.cloned.1.call-done
  1370.1 61.7 %reduce-scatter.70.cloned.1.call-done = bf16[128,256]{1,0:T(8,128)(2,1)} async-done(((bf16[1024,256]{1,0:T(8,128)(2,1)}), bf16[128,256]{1,0:T(8,128)(2,1)}) %reduce-scatter.70.cloned.1.call-update) | async-done | bytes 65552
  1433.5 63.4 %reduce-scatter.64.cloned.1.call-done = bf16[128,256]{1,0:T(8,128)(2,1)} async-done(((bf16[1024,256]{1,0:T(8,128)(2,1)}), bf16[128,256]{1,0:T(8,128)(2,1)}) %reduce-scatter.64.cloned.1.call-update) | async-done | bytes 65552 | tf_op jit(solution)/shard_map/reduce_scatter | solution.py:292
  1498.3 63.3 %reduce-scatter.66.cloned.1.call-done = bf16[128,256]{1,0:T(8,128)(2,1)} async-done(((bf16[1024,256]{1,0:T(8,128)(2,1)}), bf16[128,256]{1,0:T(8,128)(2,1)}) %reduce-scatter.66.cloned.1.call-update) | async-done | bytes 65552 | tf_op jit(solution)/shard_map/reduce_scatter | solution.py:295
  1563.1 63.3 %reduce-scatter.68.cloned.1.call-done = bf16[128,256]{1,0:T(8,128)(2,1)} async-done(((bf16[1024,256]{1,0:T(8,128)(2,1)}), bf16[128,256]{1,0:T(8,128)(2,1)}) %reduce-scatter.68.cloned.1.call-update) | async-done | bytes 65552 | tf_op jit(solution)/shard_map/reduce_scatter | solution.py:298
  1628.0 40.0 %all-reduce = (f32[1024]{0:T(1024)}, f32[1024]{0:T(1024)}) all-reduce(f32[1024]{0:T(1024)S(1)} %add_add_fusion.5, f32[1024]{0:T(1024)S(1)} %add_add_fusion.4), channel_id=1, replica_groups=mesh['row'=8,'col'=4] {'row','col'}, use_global_device_ids=true, to_apply=%region_64.69 | all-reduce | flops 2048 | bytes 16384 | tf_op jit(solution)/shard_map/psum | solution.py:314
  1672.7 7.4 all-gather.56.cloned.1.call-done
  1682.8 15.6 all-gather.52.cloned.1.call-done
  (936 shorter events, 299.4 us)
Async XLA Ops:
  7.2 150.8 %all-gather.74.cloned.1.call-start = ((), (), s32[]{:S(2)}) async-start(), calls=%async_computation.61 | async-start | bytes 1310720 | tf_op jit(solution)/shard_map/all_gather | solution.py:133
  9.5 153.6 %all-gather.76.cloned.1.call-start = ((), (), s32[]{:S(2)}) async-start(), calls=%async_computation.62 | async-start | bytes 1310720 | tf_op jit(solution)/shard_map/all_gather | solution.py:133
  10.3 158.0 %all-gather.78.cloned.1.call-start = ((), (), s32[]{:S(2)}) async-start(), calls=%async_computation.63 | async-start | bytes 1310720 | tf_op jit(solution)/shard_map/all_gather | solution.py:133
  11.0 163.1 %all-gather.80.cloned.1.call-start = ((), (), s32[]{:S(2)}) async-start(), calls=%async_computation.64 | async-start | bytes 1310720 | tf_op jit(solution)/shard_map/all_gather | solution.py:133
  11.6 112.5 %copy-start.113 = (bf16[4,256,512]{2,1,0:T(8,128)(2,1)S(1)}, bf16[4,256,512]{2,1,0:T(8,128)(2,1)}, u32[]{:S(2)}) copy-start(bf16[4,256,512]{2,1,0:T(8,128)(2,1)} %param.23) | copy-start | bytes 3145732
  11.6 180.9 %all-gather.82.cloned.1.call-start = ((), (), s32[]{:S(2)}) async-start(), calls=%async_computation.65 | async-start | bytes 1310720 | tf_op jit(solution)/shard_map/all_gather | solution.py:134
  12.7 209.6 %reduce-scatter.32.cloned.1.call-start = ((), (), s32[]{:S(2)}) async-start(), calls=%async_computation.23 | async-start | bytes 2621440 | tf_op jit(solution)/shard_map/reduce_scatter | solution.py:71
  15.2 146.8 %copy-start.240 = (pred[512]{0:T(512)(128)(4,1)}, pred[512]{0:T(512)(128)(4,1)S(1)}, u32[]{:S(2)}) copy-start(pred[512]{0:T(512)(128)(4,1)S(1)} %compare_and_fusion.11) | copy-start | bytes 1540
  17.7 149.5 %copy-start.237 = (pred[512]{0:T(512)(128)(4,1)}, pred[512]{0:T(512)(128)(4,1)S(1)}, u32[]{:S(2)}) copy-start(pred[512]{0:T(512)(128)(4,1)S(1)} %compare_and_fusion.9) | copy-start | bytes 1540
  24.0 133.9 %copy-start.216 = (s32[1024]{0:T(1024)}, s32[1024]{0:T(1024)S(1)}, u32[]{:S(2)}) copy-start(s32[1024]{0:T(1024)S(1)} %pad_clamp_fusion.11) | copy-start | bytes 12292
  24.1 139.1 %copy-start.208 = (s32[1024]{0:T(1024)}, s32[1024]{0:T(1024)S(1)}, u32[]{:S(2)}) copy-start(s32[1024]{0:T(1024)S(1)} %pad_clamp_fusion.9) | copy-start | bytes 12292
  24.1 144.2 %copy-start.210 = (s32[1024]{0:T(1024)}, s32[1024]{0:T(1024)S(1)}, u32[]{:S(2)}) copy-start(s32[1024]{0:T(1024)S(1)} %pad_clamp_fusion.7) | copy-start | bytes 12292
  58.8 129.1 %copy-start.72 = (pred[512,512]{0,1:T(8,128)(4,1)}, pred[512,512]{0,1:T(8,128)(4,1)S(1)}, u32[]{:S(2)}) copy-start(pred[512,512]{0,1:T(8,128)(4,1)S(1)} %fusion.43) | copy-start | bytes 786436
  183.5 244.4 %copy-start.2 = (bf16[512,1024]{1,0:T(8,128)(2,1)}, bf16[512,1024]{1,0:T(8,128)(2,1)S(1)}, u32[]{:S(2)}) copy-start(bf16[512,1024]{1,0:T(8,128)(2,1)S(1)} %get-tuple-element.426) | copy-start | bytes 3145732
  183.5 255.2 %copy-start = (bf16[512,1024]{1,0:T(8,128)(2,1)}, bf16[512,1024]{1,0:T(8,128)(2,1)S(1)}, u32[]{:S(2)}) copy-start(bf16[512,1024]{1,0:T(8,128)(2,1)S(1)} %get-tuple-element.427) | copy-start | bytes 3145732
  191.7 75.6 %all-gather.38.cloned.1.call-start = ((), (), s32[]{:S(2)}) async-start(), calls=%async_computation.25 | async-start | bytes 1622016 | tf_op jit(solution)/shard_map/all_gather | solution.py:123
  192.4 91.9 %all-gather.36.cloned.1.call-start = ((), (), s32[]{:S(2)}) async-start(), calls=%async_computation.24 | async-start | bytes 1310720 | tf_op jit(solution)/shard_map/all_gather | solution.py:67
  223.6 189.7 %copy-start.227 = (f32[128]{0:T(128)}, f32[128]{0:T(128)S(1)}, u32[]{:S(2)}) copy-start(f32[128]{0:T(128)S(1)} %add_rsqrt_fusion.7) | copy-start | bytes 1540
  225.2 104.2 %all-gather.40.cloned.1.call-start = ((), (), s32[]{:S(2)}) async-start(), calls=%async_computation.26 | async-start | bytes 1622016 | tf_op jit(solution)/shard_map/all_gather | solution.py:124
  226.0 146.5 %all-gather.42.cloned.1.call-start = ((), (), s32[]{:S(2)}) async-start(), calls=%async_computation.27 | async-start | bytes 1622016 | tf_op jit(solution)/shard_map/all_gather | solution.py:125
  226.5 184.8 %reduce-scatter.48.cloned.1.call-start = ((), (), s32[]{:S(2)}) async-start(), calls=%async_computation.42 | async-start | bytes 2621440 | tf_op jit(solution)/shard_map/reduce_scatter | solution.py:71
  381.8 76.0 %all-gather.58.cloned.1.call-start = ((), (), s32[]{:S(2)}) async-start(), calls=%async_computation.43 | async-start | bytes 1310720 | tf_op jit(solution)/shard_map/all_gather | solution.py:67
  415.5 62.9 %all-gather.88.cloned.1.call-start = ((), (), s32[]{:S(2)}) async-start(), calls=%async_computation.68 | async-start | bytes 1310720 | tf_op jit(solution)/shard_map/all_gather | solution.py:134
  416.2 67.0 %all-gather.86.cloned.1.call-start = ((), (), s32[]{:S(2)}) async-start(), calls=%async_computation.67 | async-start | bytes 1310720 | tf_op jit(solution)/shard_map/all_gather | solution.py:134
  416.8 71.3 %all-gather.84.cloned.1.call-start = ((), (), s32[]{:S(2)}) async-start(), calls=%async_computation.66 | async-start | bytes 1310720 | tf_op jit(solution)/shard_map/all_gather | solution.py:134
  417.4 103.1 %reduce-scatter.36.cloned.1.call-start = ((), (), s32[]{:S(2)}) async-start(), calls=%async_computation.30 | async-start | bytes 2621440 | tf_op jit(solution)/shard_map/reduce_scatter | solution.py:71
  432.3 122.4 %reduce-scatter.40.cloned.1.call-start = ((), (), s32[]{:S(2)}) async-start(), calls=%async_computation.34 | async-start | bytes 2621440 | tf_op jit(solution)/shard_map/reduce_scatter | solution.py:71
  443.7 144.5 %reduce-scatter.44.cloned.1.call-start = ((), (), s32[]{:S(2)}) async-start(), calls=%async_computation.38 | async-start | bytes 2621440 | tf_op jit(solution)/shard_map/reduce_scatter | solution.py:71
  457.7 164.3 %reduce-scatter.50.cloned.1.call-start = ((), (), s32[]{:S(2)}) async-start(), calls=%async_computation.44 | async-start | bytes 2621440 | tf_op jit(solution)/shard_map/reduce_scatter | solution.py:71
  472.0 183.6 %reduce-scatter.34.cloned.1.call-start = ((), (), s32[]{:S(2)}) async-start(), calls=%async_computation.28 | async-start | bytes 2621440 | tf_op jit(solution)/shard_map/reduce_scatter | solution.py:71
  476.9 198.8 %all-gather.46.cloned.1.call-start = ((), (), s32[]{:S(2)}) async-start(), calls=%async_computation.31 | async-start | bytes 1310720 | tf_op jit(solution)/shard_map/all_gather | solution.py:67
  589.6 325.5 %copy-start.28 = (f32[128,1024]{1,0:T(8,128)}, f32[128,1024]{1,0:T(8,128)S(1)}, u32[]{:S(2)}) copy-start(f32[128,1024]{1,0:T(8,128)S(1)} %get-tuple-element.325) | copy-start | bytes 1572868
  658.8 58.5 %reduce-scatter.52.cloned.1.call-start = ((), (), s32[]{:S(2)}) async-start(), calls=%async_computation.46 | async-start | bytes 2621440 | tf_op jit(solution)/shard_map/reduce_scatter | solution.py:71
  686.0 53.3 %all-gather.62.cloned.1.call-start = ((), (), s32[]{:S(2)}) async-start(), calls=%async_computation.47 | async-start | bytes 1310720 | tf_op jit(solution)/shard_map/all_gather | solution.py:67
  722.5 35.1 %all-gather.54.cloned.1.call-start = ((), (), s32[]{:S(2)}) async-start(), calls=%async_computation.39 | async-start | bytes 1310720 | tf_op jit(solution)/shard_map/all_gather | solution.py:67
  723.1 52.7 %all-gather.50.cloned.1.call-start = ((), (), s32[]{:S(2)}) async-start(), calls=%async_computation.35 | async-start | bytes 1310720 | tf_op jit(solution)/shard_map/all_gather | solution.py:67
  723.8 86.1 %reduce-scatter.54.cloned.1.call-start = ((), (), s32[]{:S(2)}) async-start(), calls=%async_computation.48 | async-start | bytes 2621440 | tf_op jit(solution)/shard_map/reduce_scatter | solution.py:71
  753.3 90.2 %reduce-scatter.38.cloned.1.call-start = ((), (), s32[]{:S(2)}) async-start(), calls=%async_computation.32 | async-start | bytes 2621440 | tf_op jit(solution)/shard_map/reduce_scatter | solution.py:71
  757.4 119.9 %reduce-scatter.60.cloned.1.call-start = ((), (), s32[]{:S(2)}) async-start(), calls=%async_computation.54 | async-start | bytes 2621440 | tf_op jit(solution)/shard_map/reduce_scatter | solution.py:71
  767.9 143.1 %reduce-scatter.56.cloned.1.call-start = ((), (), s32[]{:S(2)}) async-start(), calls=%async_computation.50 | async-start | bytes 2621440 | tf_op jit(solution)/shard_map/reduce_scatter | solution.py:71
  786.2 148.2 %all-gather.66.cloned.1.call-start = ((), (), s32[]{:S(2)}) async-start(), calls=%async_computation.51 | async-start | bytes 1310720 | tf_op jit(solution)/shard_map/all_gather | solution.py:67
  917.5 36.3 %all-gather.70.cloned.1.call-start = ((), (), s32[]{:S(2)}) async-start(), calls=%async_computation.55 | async-start | bytes 1310720 | tf_op jit(solution)/shard_map/all_gather | solution.py:67
  918.2 97.0 %reduce-scatter.58.cloned.1.call-start = ((), (), s32[]{:S(2)}) async-start(), calls=%async_computation.52 | async-start | bytes 2621440 | tf_op jit(solution)/shard_map/reduce_scatter | solution.py:71
  948.5 72.0 %reduce-scatter.42.cloned.1.call-start = ((), (), s32[]{:S(2)}) async-start(), calls=%async_computation.36 | async-start | bytes 2621440 | tf_op jit(solution)/shard_map/reduce_scatter | solution.py:71
  953.3 101.6 %reduce-scatter.62.cloned.1.call-start = ((), (), s32[]{:S(2)}) async-start(), calls=%async_computation.56 | async-start | bytes 2621440 | tf_op jit(solution)/shard_map/reduce_scatter | solution.py:71
  966.7 121.9 %reduce-scatter.46.cloned.1.call-start = ((), (), s32[]{:S(2)}) async-start(), calls=%async_computation.40 | async-start | bytes 2621440 | tf_op jit(solution)/shard_map/reduce_scatter | solution.py:71
  971.6 135.7 %all-gather.60.cloned.1.call-start = ((), (), s32[]{:S(2)}) async-start(), calls=%async_computation.45 | async-start | bytes 1310720 | tf_op jit(solution)/shard_map/all_gather | solution.py:282
  972.2 153.9 %all-gather.44.cloned.1.call-start = ((), (), s32[]{:S(2)}) async-start(), calls=%async_computation.29 | async-start | bytes 1310720 | tf_op jit(solution)/shard_map/all_gather | solution.py:279
  972.8 222.3 %reduce-scatter.72.cloned.1.call-start = ((), (), s32[]{:S(2)}) async-start(), calls=%async_computation.70 | async-start | bytes 1769472
  979.7 283.1 %reduce-scatter.74.cloned.1.call-start = ((), (), s32[]{:S(2)}) async-start(), calls=%async_computation.71 | async-start | bytes 1769472
  987.3 343.3 %reduce-scatter.76.cloned.1.call-start = ((), (), s32[]{:S(2)}) async-start(), calls=%async_computation.72 | async-start | bytes 1769472
  994.2 353.5 %all-gather.64.cloned.1.call-start = ((), (), s32[]{:S(2)}) async-start(), calls=%async_computation.49 | async-start | bytes 1310720 | tf_op jit(solution)/shard_map/all_gather | solution.py:282
  995.0 371.0 %all-gather.48.cloned.1.call-start = ((), (), s32[]{:S(2)}) async-start(), calls=%async_computation.33 | async-start | bytes 1310720 | tf_op jit(solution)/shard_map/all_gather | solution.py:279
  995.7 436.1 %reduce-scatter.70.cloned.1.call-start = ((), (), s32[]{:S(2)}) async-start(), calls=%async_computation.69 | async-start | bytes 589824
  1000.7 496.1 %reduce-scatter.64.cloned.1.call-start = ((), (), s32[]{:S(2)}) async-start(), calls=%async_computation.58 | async-start | bytes 589824 | tf_op jit(solution)/shard_map/reduce_scatter | solution.py:292
  1005.1 556.5 %reduce-scatter.66.cloned.1.call-start = ((), (), s32[]{:S(2)}) async-start(), calls=%async_computation.59 | async-start | bytes 589824 | tf_op jit(solution)/shard_map/reduce_scatter | solution.py:295
  1009.7 616.8 %reduce-scatter.68.cloned.1.call-start = ((), (), s32[]{:S(2)}) async-start(), calls=%async_computation.60 | async-start | bytes 589824 | tf_op jit(solution)/shard_map/reduce_scatter | solution.py:298
  1015.1 652.9 %all-gather.72.cloned.1.call-start = ((), (), s32[]{:S(2)}) async-start(), calls=%async_computation.57 | async-start | bytes 1310720 | tf_op jit(solution)/shard_map/all_gather | solution.py:282
  1091.0 579.3 %all-gather.68.cloned.1.call-start = ((), (), s32[]{:S(2)}) async-start(), calls=%async_computation.53 | async-start | bytes 1310720 | tf_op jit(solution)/shard_map/all_gather | solution.py:282
  1091.6 588.6 %all-gather.56.cloned.1.call-start = ((), (), s32[]{:S(2)}) async-start(), calls=%async_computation.41 | async-start | bytes 1310720 | tf_op jit(solution)/shard_map/all_gather | solution.py:279
  1092.1 606.3 %all-gather.52.cloned.1.call-start = ((), (), s32[]{:S(2)}) async-start(), calls=%async_computation.37 | async-start | bytes 1310720 | tf_op jit(solution)/shard_map/all_gather | solution.py:279
  1128.4 204.0 %copy-start.48 = (f32[4,64,512]{2,1,0:T(8,128)S(1)}, f32[4,64,512]{2,1,0:T(8,128)}, u32[]{:S(2)}) copy-start(f32[4,64,512]{2,1,0:T(8,128)} %copy-done.46) | copy-start | bytes 1572868
  1350.0 278.0 %copy-start.219 = (f32[1024]{0:T(1024)S(1)}, f32[1024]{0:T(1024)}, u32[]{:S(2)}) copy-start(f32[1024]{0:T(1024)} %get-tuple-element.283) | copy-start | bytes 12292
  1350.0 278.0 %copy-start.221 = (f32[1024]{0:T(1024)S(1)}, f32[1024]{0:T(1024)}, u32[]{:S(2)}) copy-start(f32[1024]{0:T(1024)} %get-tuple-element.270) | copy-start | bytes 12292
  (251 other events, 1631.2 us)
Sparse Core Ops, SparseCore 0:
  10.1 19.4 all-gather.73
  31.7 16.6 all-gather.75
  50.6 16.6 all-gather.77
  69.3 16.6 all-gather.79
  88.0 16.6 all-gather.81
  191.8 30.3 reduce-scatter.31
  224.3 42.9 all-gather.37
  269.4 14.8 all-gather.35
  286.4 42.9 all-gather.39
  331.3 41.1 all-gather.41
  381.9 29.3 reduce-scatter.47
  415.6 16.6 all-gather.57
  433.9 16.6 all-gather.87
  452.1 16.6 all-gather.85
  470.2 16.6 all-gather.83
  489.3 31.1 reduce-scatter.35
  523.5 31.1 reduce-scatter.39
  557.1 31.1 reduce-scatter.43
  590.8 31.1 reduce-scatter.49
  624.4 31.1 reduce-scatter.33
  659.0 16.6 all-gather.45
  686.1 31.1 reduce-scatter.51
  722.6 16.6 all-gather.61
  740.7 16.7 all-gather.53
  759.1 16.6 all-gather.49
  778.7 31.1 reduce-scatter.53
  812.3 31.1 reduce-scatter.37
  846.0 31.1 reduce-scatter.59
  879.8 31.1 reduce-scatter.55
  917.6 16.6 all-gather.65
  936.5 16.6 all-gather.69
  955.7 31.1 reduce-scatter.57
  989.3 31.1 reduce-scatter.41
  1023.6 31.1 reduce-scatter.61
  1057.4 31.1 reduce-scatter.45
  1090.6 16.6 all-gather.59
  1109.3 16.6 all-gather.43
  1129.4 65.5 reduce-scatter.71
  1198.3 64.4 reduce-scatter.73
  1266.2 64.3 reduce-scatter.75
  1332.1 15.4 all-gather.63
  1349.3 16.6 all-gather.47
  1369.2 62.6 reduce-scatter.69
  1435.2 61.6 reduce-scatter.63
  1500.0 61.5 reduce-scatter.65
  1564.8 61.5 reduce-scatter.67
  1627.9 15.7 all-gather.71
  1645.1 16.9 all-gather.67
  1663.5 16.6 all-gather.55
  1681.7 16.6 all-gather.51
where the time goes:
time: 1720 us; the launch traced here: 1710 us
  waiting for transfers between devices  1140 us (66%)
  blocking collectives  166 us (10%)
  matrix products  148 us (9%)
  local copies, waits for them, and re-layouts  131 us (8%)
  other arithmetic  99.4 us (6%)
  between operations  18.5 us (1%)
    reduce_scatter x16, waiting for transfers between devices, reduce_tokens(): return lax.psum_scatter(values, 'col', scatter_dimension=0, tiled=True)  417 us
    unnamed x54, waiting for transfers between devices  270 us
    all_gather x8, waiting for transfers between devices, spread_tokens(): return lax.all_gather(values, 'col', axis=0, tiled=True)  72.8 us
    reduce_scatter x1, waiting for transfers between devices, body(): lax.psum_scatter(grads_full[0].astype(jnp.bfloat16), 'row', scatter_dimen...  63.4 us
    reduce_scatter x1, waiting for transfers between devices, body(): lax.psum_scatter(grads_full[1].astype(jnp.bfloat16), 'row', scatter_dimen...  63.3 us
    reduce_scatter x1, waiting for transfers between devices, body(): lax.psum_scatter(grads_full[2].astype(jnp.bfloat16), 'row', scatter_dimen...  63.3 us
    all_gather x4, waiting for transfers between devices, body(): lax.all_gather(packed_out.astype(jnp.float32).astype(jnp.bfloat16), 'col'...  55.5 us
    dot_general x28, matrix products, product(): return jnp.dot(left, right, preferred_element_type=jnp.float32)  46.7 us
  transfers between devices with their start and end apart: 50, of which 37 were waited for; matrix products, arithmetic and copies ran while one was open for 18% of the time, Pallas kernels for 0%

commit v1 on v0

--- a/solution.py
+++ b/solution.py
@@ -9,6 +9,27 @@
 MICRO = 4
 EPSILON = 1e-06
 MASKED = -1e30
+
+
+def gather_around(x, axis, dim):
+    size, index, rows = (lax.axis_size(axis), lax.axis_index(axis), x.shape[dim])
+    forward = [(i, (i + 1) % size) for i in range(size)]
+    downward = [(i, (i - 1) % size) for i in range(size)]
+    out = jnp.zeros((*x.shape[:dim], size * rows, *x.shape[dim + 1 :]), x.dtype)
+    out = lax.dynamic_update_slice_in_dim(out, x, index * rows, axis=dim)
+    from_left = from_right = x
+    half = size // 2
+    for step in range(1, half + 1):
+        from_left = lax.ppermute(from_left, axis, forward)
+        out = lax.dynamic_update_slice_in_dim(
+            out, from_left, (index - step) % size * rows, axis=dim
+        )
+        if step < size - half:
+            from_right = lax.ppermute(from_right, axis, downward)
+            out = lax.dynamic_update_slice_in_dim(
+                out, from_right, (index + step) % size * rows, axis=dim
+            )
+    return out
 
 
 def product(left, right):
@@ -64,7 +85,7 @@
 
 
 def spread_tokens(values):
-    return lax.all_gather(values, "col", axis=0, tiled=True)
+    return gather_around(values, "col", 0)
 
 
 def reduce_tokens(values):

time: 1720 us -> 1560 us (0.907)
  waiting for transfers between devices: 1140 us -> 964 us
  local copies, waits for them, and re-layouts: 131 us -> 151 us
    reduce_scatter x16, waiting for transfers between devices: 417 us -> 253 us  [reduce_tokens(): return lax.psum_scatter(values, 'col', scatter_dimension=0, tiled=True)]
    all_gather x8 -> x0, waiting for transfers between devices: 72.8 us -> none  [spread_tokens(): return lax.all_gather(values, 'col', axis=0, tiled=True)]
    ppermute x0 -> x24, waiting for transfers between devices: none -> 62.7 us  [the longest x16 62.4 us: gather_around(): from_left = lax.ppermute(from_left, axis, forward)]
    unnamed x54 -> x46, waiting for transfers between devices: 270 us -> 256 us
    unnamed x543 -> x579, local copies, waits for them, and re-layouts: 43.7 us -> 49 us
  transfers between devices with their start and end apart: 50 -> 66, of which waited for: 37 -> 43; matrix products, arithmetic and copies ran while one was open for 18% -> 22% of each run, Pallas kernels for 0% -> 0%
where the time goes in v1:
time: 1560 us; the launch traced here: 1550 us
  waiting for transfers between devices  964 us (62%)
  blocking collectives  167 us (11%)
  local copies, waits for them, and re-layouts  151 us (10%)
  matrix products  138 us (9%)
  other arithmetic  92.4 us (6%)
  between operations  18.8 us (1%)
  starting transfers between devices  18.5 us (1%)
    unnamed x46, waiting for transfers between devices  256 us
    reduce_scatter x16, waiting for transfers between devices, reduce_tokens(): return lax.psum_scatter(values, 'col', scatter_dimension=0, tiled=True)  253 us
    reduce_scatter x1, waiting for transfers between devices, body(): lax.psum_scatter(grads_full[0].astype(jnp.bfloat16), 'row', scatter_dimen...  63.6 us
    reduce_scatter x1, waiting for transfers between devices, body(): lax.psum_scatter(grads_full[1].astype(jnp.bfloat16), 'row', scatter_dimen...  63.5 us
    reduce_scatter x1, waiting for transfers between devices, body(): lax.psum_scatter(grads_full[2].astype(jnp.bfloat16), 'row', scatter_dimen...  63.4 us
    all_gather x4, waiting for transfers between devices, body(): lax.all_gather(packed_out.astype(jnp.float32).astype(jnp.bfloat16), 'col'...  63.2 us
    ppermute x16, waiting for transfers between devices, gather_around(): from_left = lax.ppermute(from_left, axis, forward)  62.4 us
    unnamed x579, local copies, waits for them, and re-layouts  49 us
  transfers between devices with their start and end apart: 66, of which 43 were waited for; matrix products, arithmetic and copies ran while one was open for 22% of the time, Pallas kernels for 0%

profile of v1, /device:TPU:0, one launch (start us, length us, event | category | flops | bytes accessed | tf_op | source)
XLA Modules:
  0.0 1550.2 jit_solution(268541260761328087)
XLA Ops:
  24.2 33.2 %all_gather.92 = bf16[1024,256]{1,0:T(8,128)(2,1)S(1)} all-gather(bf16[128,256]{1,0:T(8,128)(2,1)S(1)} %copy-done.211), channel_id=1, replica_groups=mesh['row'=8,'col'=4] {'row'}, dimensions={0}, use_global_device_ids=true | all-gather | bytes 589824 | tf_op jit(solution)/shard_map/all_gather | solution.py:140
  58.6 31.5 %all_gather.93 = bf16[1024,256]{1,0:T(8,128)(2,1)S(1)} all-gather(bf16[128,256]{1,0:T(8,128)(2,1)S(1)} %copy-done.212), channel_id=1, replica_groups=mesh['row'=8,'col'=4] {'row'}, dimensions={0}, use_global_device_ids=true | all-gather | bytes 589824 | tf_op jit(solution)/shard_map/all_gather | solution.py:141
  90.2 33.4 %all_gather.91 = bf16[1024,256]{1,0:T(8,128)(2,1)} all-gather(bf16[128,256]{1,0:T(8,128)(2,1)S(1)} %copy-done.213), channel_id=1, replica_groups=mesh['row'=8,'col'=4] {'row'}, dimensions={0}, use_global_device_ids=true | all-gather | bytes 589824 | tf_op jit(solution)/shard_map/all_gather | solution.py:142
  124.5 28.3 %all_gather.94 = bf16[256,1024]{1,0:T(8,128)(2,1)} all-gather(bf16[256,128]{1,0:T(8,128)(2,1)S(1)} %copy-done.214), channel_id=1, replica_groups=mesh['row'=8,'col'=4] {'row'}, dimensions={1}, use_global_device_ids=true | all-gather | bytes 589824 | tf_op jit(solution)/shard_map/all_gather | solution.py:143
  157.4 4.1 gather_fusion
  162.6 4.1 gather_fusion.3
  167.8 4.1 gather_fusion.6
  172.9 4.2 gather_fusion.9
  178.3 4.1 multiply_convert_fusion.7
  208.6 5.3 gather_fusion.12
  213.9 3.2 broadcast_select_fusion.3
  217.1 4.3 reduce-scatter.32.cloned.1.call-done
  225.7 6.3 collective-permute-done
  232.0 34.5 %all-gather.32.cloned.1.call-done = bf16[704,1024]{1,0:T(8,128)(2,1)} async-done(((bf16[704,128]{1,0:T(8,128)(2,1)}), bf16[704,1024]{1,0:T(8,128)(2,1)}) %all-gather.32.cloned.1.call-update) | async-done | bytes 1441808 | tf_op jit(solution)/shard_map/all_gather | solution.py:146
  266.5 3.7 fusion.143
  273.2 36.6 %all-gather.30.cloned.1.call-done = bf16[1024,704]{0,1:T(8,128)(2,1)} async-done(((bf16[128,704]{0,1:T(8,128)(2,1)}), bf16[1024,704]{0,1:T(8,128)(2,1)}) %all-gather.30.cloned.1.call-update) | async-done | bytes 1441808 | tf_op jit(solution)/shard_map/all_gather | solution.py:145
  309.7 3.4 fusion.126
  313.1 39.8 %all-gather.28.cloned.1.call-done = bf16[1024,704]{0,1:T(8,128)(2,1)} async-done(((bf16[128,704]{0,1:T(8,128)(2,1)}), bf16[1024,704]{0,1:T(8,128)(2,1)}) %all-gather.28.cloned.1.call-update) | async-done | bytes 1441808 | tf_op jit(solution)/shard_map/all_gather | solution.py:144
  353.0 4.8 multiply_convert_fusion.14
  362.1 7.2 all-gather.60.cloned.1.call-done
  369.3 4.9 gather_fusion.14
  374.2 3.2 broadcast_select_fusion.2
  377.4 25.6 %reduce-scatter.36.cloned.1.call-done = f32[128,1024]{1,0:T(8,128)} async-done(((f32[512,1024]{1,0:T(8,128)}), f32[128,1024]{1,0:T(8,128)}) %reduce-scatter.36.cloned.1.call-update) | async-done | bytes 524304 | tf_op jit(solution)/shard_map/reduce_scatter | solution.py:92
  407.3 6.2 collective-permute-done.3
  414.7 4.7 collective-permute-done.5
  453.6 17.4 %reduce-scatter.52.cloned.1.call-done = f32[128,1024]{1,0:T(8,128)} async-done(((f32[512,1024]{1,0:T(8,128)}), f32[128,1024]{1,0:T(8,128)}) %reduce-scatter.52.cloned.1.call-update) | async-done | bytes 524304 | tf_op jit(solution)/shard_map/reduce_scatter | solution.py:92
  481.3 3.9 collective-permute-done.12
  490.8 5.0 collective-permute-done.14
  515.8 3.9 multiply_reduce_fusion.2
  529.0 3.7 fusion.127
  533.4 4.9 gather_fusion.18
  545.8 6.8 collective-permute-done.9
  553.8 4.7 collective-permute-done.11
  566.9 4.9 gather_fusion.16
  571.8 3.2 broadcast_select_fusion.1
  575.0 4.6 reduce-scatter.40.cloned.1.call-done
  583.2 6.2 collective-permute-done.6
  590.4 4.7 collective-permute-done.8
  605.7 7.4 reduce-scatter.50.cloned.1.call-done
  613.2 33.7 %reduce-scatter.54.cloned.1.call-done = f32[128,1024]{1,0:T(8,128)} async-done(((f32[512,1024]{1,0:T(8,128)}), f32[128,1024]{1,0:T(8,128)}) %reduce-scatter.54.cloned.1.call-update) | async-done | bytes 524304 | tf_op jit(solution)/shard_map/reduce_scatter | solution.py:92
  650.6 29.9 %reduce-scatter.34.cloned.1.call-done = f32[128,1024]{1,0:T(8,128)} async-done(((f32[512,1024]{1,0:T(8,128)}), f32[128,1024]{1,0:T(8,128)}) %reduce-scatter.34.cloned.1.call-update) | async-done | bytes 524304 | tf_op jit(solution)/shard_map/reduce_scatter | solution.py:92
  680.4 34.3 %reduce-scatter.60.cloned.1.call-done = f32[128,1024]{1,0:T(8,128)} async-done(((f32[512,1024]{1,0:T(8,128)}), f32[128,1024]{1,0:T(8,128)}) %reduce-scatter.60.cloned.1.call-update) | async-done | bytes 524304 | tf_op jit(solution)/shard_map/reduce_scatter | solution.py:92
  714.7 33.7 %reduce-scatter.56.cloned.1.call-done = f32[128,1024]{1,0:T(8,128)} async-done(((f32[512,1024]{1,0:T(8,128)}), f32[128,1024]{1,0:T(8,128)}) %reduce-scatter.56.cloned.1.call-update) | async-done | bytes 524304 | tf_op jit(solution)/shard_map/reduce_scatter | solution.py:92
  748.4 3.9 subtract_convert_fusion.3
  781.7 8.4 collective-permute-done.20
  792.5 3.9 multiply_reduce_fusion.1
  804.8 3.8 fusion.142
  861.1 3.4 subtract_convert_fusion.2
  864.6 30.1 %reduce-scatter.46.cloned.1.call-done = f32[128,1024]{1,0:T(8,128)} async-done(((f32[512,1024]{1,0:T(8,128)}), f32[128,1024]{1,0:T(8,128)}) %reduce-scatter.46.cloned.1.call-update) | async-done | bytes 524304 | tf_op jit(solution)/shard_map/reduce_scatter | solution.py:92
  897.3 30.9 %reduce-scatter.42.cloned.1.call-done = f32[128,1024]{1,0:T(8,128)} async-done(((f32[512,1024]{1,0:T(8,128)}), f32[128,1024]{1,0:T(8,128)}) %reduce-scatter.42.cloned.1.call-update) | async-done | bytes 524304 | tf_op jit(solution)/shard_map/reduce_scatter | solution.py:92
  932.8 64.5 %reduce-scatter.72.cloned.1.call-done = bf16[128,704]{1,0:T(8,128)(2,1)} async-done(((bf16[1024,704]{1,0:T(8,128)(2,1)}), bf16[128,704]{1,0:T(8,128)(2,1)}) %reduce-scatter.72.cloned.1.call-update) | async-done | bytes 180240
  999.1 66.0 %reduce-scatter.74.cloned.1.call-done = bf16[128,704]{1,0:T(8,128)(2,1)} async-done(((bf16[1024,704]{1,0:T(8,128)(2,1)}), bf16[128,704]{1,0:T(8,128)(2,1)}) %reduce-scatter.74.cloned.1.call-update) | async-done | bytes 180240
  1067.0 66.0 %reduce-scatter.76.cloned.1.call-done = bf16[128,704]{1,0:T(8,128)(2,1)} async-done(((bf16[1024,704]{1,0:T(8,128)(2,1)}), bf16[128,704]{1,0:T(8,128)(2,1)}) %reduce-scatter.76.cloned.1.call-update) | async-done | bytes 180240
  1147.2 50.8 %reduce-scatter.70.cloned.1.call-done = bf16[128,256]{1,0:T(8,128)(2,1)} async-done(((bf16[1024,256]{1,0:T(8,128)(2,1)}), bf16[128,256]{1,0:T(8,128)(2,1)}) %reduce-scatter.70.cloned.1.call-update) | async-done | bytes 65552
  1199.6 15.7 %all-gather.42.cloned.1.call-done = bf16[512,1024]{1,0:T(8,128)(2,1)} async-done(((bf16[128,1024]{1,0:T(8,128)(2,1)}), bf16[512,1024]{1,0:T(8,128)(2,1)}) %all-gather.42.cloned.1.call-update) | async-done | bytes 1048592 | tf_op jit(solution)/shard_map/all_gather | solution.py:303
  1217.6 15.8 %all-gather.34.cloned.1.call-done = bf16[512,1024]{1,0:T(8,128)(2,1)} async-done(((bf16[128,1024]{1,0:T(8,128)(2,1)}), bf16[512,1024]{1,0:T(8,128)(2,1)}) %all-gather.34.cloned.1.call-update) | async-done | bytes 1048592 | tf_op jit(solution)/shard_map/all_gather | solution.py:300
  1235.9 63.6 %reduce-scatter.64.cloned.1.call-done = bf16[128,256]{1,0:T(8,128)(2,1)} async-done(((bf16[1024,256]{1,0:T(8,128)(2,1)}), bf16[128,256]{1,0:T(8,128)(2,1)}) %reduce-scatter.64.cloned.1.call-update) | async-done | bytes 65552 | tf_op jit(solution)/shard_map/reduce_scatter | solution.py:313
  1301.0 63.5 %reduce-scatter.66.cloned.1.call-done = bf16[128,256]{1,0:T(8,128)(2,1)} async-done(((bf16[1024,256]{1,0:T(8,128)(2,1)}), bf16[128,256]{1,0:T(8,128)(2,1)}) %reduce-scatter.66.cloned.1.call-update) | async-done | bytes 65552 | tf_op jit(solution)/shard_map/reduce_scatter | solution.py:316
  1365.9 63.4 %reduce-scatter.68.cloned.1.call-done = bf16[128,256]{1,0:T(8,128)(2,1)} async-done(((bf16[1024,256]{1,0:T(8,128)(2,1)}), bf16[128,256]{1,0:T(8,128)(2,1)}) %reduce-scatter.68.cloned.1.call-update) | async-done | bytes 65552 | tf_op jit(solution)/shard_map/reduce_scatter | solution.py:319
  1431.9 40.5 %all-reduce = (f32[1024]{0:T(1024)}, f32[1024]{0:T(1024)}) all-reduce(f32[1024]{0:T(1024)S(1)} %add_add_fusion.5, f32[1024]{0:T(1024)S(1)} %add_add_fusion.4), channel_id=1, replica_groups=mesh['row'=8,'col'=4] {'row','col'}, use_global_device_ids=true, to_apply=%region_64.69 | all-reduce | flops 2048 | bytes 16384 | tf_op jit(solution)/shard_map/psum | solution.py:335
  1477.8 5.5 all-gather.44.cloned.1.call-done
  1485.5 16.0 %all-gather.40.cloned.1.call-done = bf16[512,1024]{1,0:T(8,128)(2,1)} async-done(((bf16[128,1024]{1,0:T(8,128)(2,1)}), bf16[512,1024]{1,0:T(8,128)(2,1)}) %all-gather.40.cloned.1.call-update) | async-done | bytes 1048592 | tf_op jit(solution)/shard_map/all_gather | solution.py:300
  1504.0 15.9 %all-gather.38.cloned.1.call-done = bf16[512,1024]{1,0:T(8,128)(2,1)} async-done(((bf16[128,1024]{1,0:T(8,128)(2,1)}), bf16[512,1024]{1,0:T(8,128)(2,1)}) %all-gather.38.cloned.1.call-update) | async-done | bytes 1048592 | tf_op jit(solution)/shard_map/all_gather | solution.py:300
  1522.7 15.4 all-gather.36.cloned.1.call-done
  (1030 shorter events, 330.6 us)
Async XLA Ops:
  7.2 150.2 %all-gather.50.cloned.1.call-start = ((), (), s32[]{:S(2)}) async-start(), calls=%async_computation.53 | async-start | bytes 1310720 | tf_op jit(solution)/shard_map/all_gather | solution.py:154
  9.5 153.1 %all-gather.52.cloned.1.call-start = ((), (), s32[]{:S(2)}) async-start(), calls=%async_computation.54 | async-start | bytes 1310720 | tf_op jit(solution)/shard_map/all_gather | solution.py:154
  10.3 157.5 %all-gather.54.cloned.1.call-start = ((), (), s32[]{:S(2)}) async-start(), calls=%async_computation.55 | async-start | bytes 1310720 | tf_op jit(solution)/shard_map/all_gather | solution.py:154
  11.0 161.9 %all-gather.56.cloned.1.call-start = ((), (), s32[]{:S(2)}) async-start(), calls=%async_computation.56 | async-start | bytes 1310720 | tf_op jit(solution)/shard_map/all_gather | solution.py:154
  11.6 196.9 %all-gather.58.cloned.1.call-start = ((), (), s32[]{:S(2)}) async-start(), calls=%async_computation.57 | async-start | bytes 1310720 | tf_op jit(solution)/shard_map/all_gather | solution.py:155
  12.6 208.8 %reduce-scatter.32.cloned.1.call-start = ((), (), s32[]{:S(2)}) async-start(), calls=%async_computation.23 | async-start | bytes 2621440 | tf_op jit(solution)/shard_map/reduce_scatter | solution.py:92
  190.7 75.8 %all-gather.32.cloned.1.call-start = ((), (), s32[]{:S(2)}) async-start(), calls=%async_computation.26 | async-start | bytes 1622016 | tf_op jit(solution)/shard_map/all_gather | solution.py:146
  191.5 118.3 %all-gather.30.cloned.1.call-start = ((), (), s32[]{:S(2)}) async-start(), calls=%async_computation.25 | async-start | bytes 1622016 | tf_op jit(solution)/shard_map/all_gather | solution.py:145
  192.2 160.8 %all-gather.28.cloned.1.call-start = ((), (), s32[]{:S(2)}) async-start(), calls=%async_computation.24 | async-start | bytes 1622016 | tf_op jit(solution)/shard_map/all_gather | solution.py:144
  193.0 176.3 %all-gather.60.cloned.1.call-start = ((), (), s32[]{:S(2)}) async-start(), calls=%async_computation.58 | async-start | bytes 1310720 | tf_op jit(solution)/shard_map/all_gather | solution.py:155
  193.5 209.5 %reduce-scatter.36.cloned.1.call-start = ((), (), s32[]{:S(2)}) async-start(), calls=%async_computation.29 | async-start | bytes 2621440 | tf_op jit(solution)/shard_map/reduce_scatter | solution.py:92
  208.4 245.2 %reduce-scatter.48.cloned.1.call-start = ((), (), s32[]{:S(2)}) async-start(), calls=%async_computation.38 | async-start | bytes 2621440 | tf_op jit(solution)/shard_map/reduce_scatter | solution.py:92
  223.9 8.1 collective-permute-start
  223.9 47.3 %collective-permute-start.1 = (bf16[128,1024]{1,0:T(8,128)(2,1)S(1)}, bf16[128,1024]{1,0:T(8,128)(2,1)}, u32[]{:S(2)}, u32[]{:S(2)}) collective-permute-start(bf16[128,1024]{1,0:T(8,128)(2,1)S(1)} %get-tuple-element.321), channel_id=1, source_target_pairs={{0,3},{1,0},{2,1},{3,2},{4,7},{5,4},{6,5},{7,6},{8,11},{9,8},{10,9... | collective-permute-start | bytes 786440 | tf_op jit(solution)/shard_map/ppermute | solution.py:28
  232.0 40.2 %collective-permute-start.2 = (bf16[128,1024]{1,0:T(8,128)(2,1)}, bf16[128,1024]{1,0:T(8,128)(2,1)}, u32[]{:S(2)}, u32[]{:S(2)}) collective-permute-start(bf16[128,1024]{1,0:T(8,128)(2,1)} %collective-permute-done), channel_id=1, source_target_pairs={{0,1},{1,2},{2,3},{3,0},{4,5},{5,6},{6,7},{7,4},{8,9},{9,10},{10,1... | collective-permute-start | bytes 786440 | tf_op jit(solution)/shard_map/ppermute | solution.py:23
  362.1 108.9 %reduce-scatter.52.cloned.1.call-start = ((), (), s32[]{:S(2)}) async-start(), calls=%async_computation.41 | async-start | bytes 2621440 | tf_op jit(solution)/shard_map/reduce_scatter | solution.py:92
  405.5 8.0 collective-permute-start.3
  405.5 9.1 collective-permute-start.4
  413.5 5.9 collective-permute-start.5
  427.3 105.5 %all-gather.64.cloned.1.call-start = ((), (), s32[]{:S(2)}) async-start(), calls=%async_computation.60 | async-start | bytes 1310720 | tf_op jit(solution)/shard_map/all_gather | solution.py:155
  427.8 113.6 %reduce-scatter.44.cloned.1.call-start = ((), (), s32[]{:S(2)}) async-start(), calls=%async_computation.35 | async-start | bytes 2621440 | tf_op jit(solution)/shard_map/reduce_scatter | solution.py:92
  442.7 123.6 %all-gather.62.cloned.1.call-start = ((), (), s32[]{:S(2)}) async-start(), calls=%async_computation.59 | async-start | bytes 1310720 | tf_op jit(solution)/shard_map/all_gather | solution.py:155
  443.3 136.3 %reduce-scatter.40.cloned.1.call-start = ((), (), s32[]{:S(2)}) async-start(), calls=%async_computation.32 | async-start | bytes 2621440 | tf_op jit(solution)/shard_map/reduce_scatter | solution.py:92
  476.9 8.3 collective-permute-start.12
  478.7 134.4 %reduce-scatter.50.cloned.1.call-start = ((), (), s32[]{:S(2)}) async-start(), calls=%async_computation.39 | async-start | bytes 2621440 | tf_op jit(solution)/shard_map/reduce_scatter | solution.py:92
  478.8 12.0 collective-permute-start.13
  485.2 10.7 collective-permute-start.14
  487.5 19.3 %collective-permute-start.15 = (bf16[128,1024]{1,0:T(8,128)(2,1)}, bf16[128,1024]{1,0:T(8,128)(2,1)}, u32[]{:S(2)}, u32[]{:S(2)}) collective-permute-start(bf16[128,1024]{1,0:T(8,128)(2,1)} %get-tuple-element.313), channel_id=1, source_target_pairs={{0,1},{1,2},{2,3},{3,0},{4,5},{5,6},{6,7},{7,4},{8,9},{9,10},{10,1... | collective-permute-start | bytes 786440 | tf_op jit(solution)/shard_map/ppermute | solution.py:23
  487.6 21.4 %collective-permute-start.16 = (bf16[128,1024]{1,0:T(8,128)(2,1)}, bf16[128,1024]{1,0:T(8,128)(2,1)}, u32[]{:S(2)}, u32[]{:S(2)}) collective-permute-start(bf16[128,1024]{1,0:T(8,128)(2,1)} %get-tuple-element.313), channel_id=1, source_target_pairs={{0,3},{1,0},{2,1},{3,2},{4,7},{5,4},{6,5},{7,6},{8,11},{9,8},{10,9... | collective-permute-start | bytes 786440 | tf_op jit(solution)/shard_map/ppermute | solution.py:28
  506.7 140.1 %reduce-scatter.54.cloned.1.call-start = ((), (), s32[]{:S(2)}) async-start(), calls=%async_computation.42 | async-start | bytes 2621440 | tf_op jit(solution)/shard_map/reduce_scatter | solution.py:92
  506.8 6.5 collective-permute-start.17
  527.9 152.5 %reduce-scatter.34.cloned.1.call-start = ((), (), s32[]{:S(2)}) async-start(), calls=%async_computation.27 | async-start | bytes 2621440 | tf_op jit(solution)/shard_map/reduce_scatter | solution.py:92
  532.7 182.0 %reduce-scatter.60.cloned.1.call-start = ((), (), s32[]{:S(2)}) async-start(), calls=%async_computation.47 | async-start | bytes 2621440 | tf_op jit(solution)/shard_map/reduce_scatter | solution.py:92
  544.0 8.6 collective-permute-start.9
  544.0 9.7 collective-permute-start.10
  566.2 182.2 %reduce-scatter.56.cloned.1.call-start = ((), (), s32[]{:S(2)}) async-start(), calls=%async_computation.44 | async-start | bytes 2621440 | tf_op jit(solution)/shard_map/reduce_scatter | solution.py:92
  581.4 8.0 collective-permute-start.6
  581.4 9.0 collective-permute-start.7
  602.9 257.5 %reduce-scatter.38.cloned.1.call-start = ((), (), s32[]{:S(2)}) async-start(), calls=%async_computation.30 | async-start | bytes 2621440 | tf_op jit(solution)/shard_map/reduce_scatter | solution.py:92
  755.5 6.1 collective-permute-start.21
  757.8 102.6 %reduce-scatter.62.cloned.1.call-start = ((), (), s32[]{:S(2)}) async-start(), calls=%async_computation.48 | async-start | bytes 2621440 | tf_op jit(solution)/shard_map/reduce_scatter | solution.py:92
  757.9 8.8 collective-permute-start.22
  761.6 6.0 collective-permute-start.23
  763.8 14.1 collective-permute-start.18
  764.3 15.8 %collective-permute-start.19 = (bf16[128,1024]{1,0:T(8,128)(2,1)}, bf16[128,1024]{1,0:T(8,128)(2,1)}, u32[]{:S(2)}, u32[]{:S(2)}) collective-permute-start(bf16[128,1024]{1,0:T(8,128)(2,1)} %get-tuple-element.315), channel_id=1, source_target_pairs={{0,3},{1,0},{2,1},{3,2},{4,7},{5,4},{6,5},{7,6},{8,11},{9,8},{10,9... | collective-permute-start | bytes 786440 | tf_op jit(solution)/shard_map/ppermute | solution.py:28
  777.8 83.2 %reduce-scatter.58.cloned.1.call-start = ((), (), s32[]{:S(2)}) async-start(), calls=%async_computation.45 | async-start | bytes 2621440 | tf_op jit(solution)/shard_map/reduce_scatter | solution.py:92
  777.9 12.2 collective-permute-start.20
  803.6 91.1 %reduce-scatter.46.cloned.1.call-start = ((), (), s32[]{:S(2)}) async-start(), calls=%async_computation.36 | async-start | bytes 2621440 | tf_op jit(solution)/shard_map/reduce_scatter | solution.py:92
  808.6 119.6 %reduce-scatter.42.cloned.1.call-start = ((), (), s32[]{:S(2)}) async-start(), calls=%async_computation.33 | async-start | bytes 2621440 | tf_op jit(solution)/shard_map/reduce_scatter | solution.py:92
  812.1 185.2 %reduce-scatter.72.cloned.1.call-start = ((), (), s32[]{:S(2)}) async-start(), calls=%async_computation.62 | async-start | bytes 1769472
  822.6 242.6 %reduce-scatter.74.cloned.1.call-start = ((), (), s32[]{:S(2)}) async-start(), calls=%async_computation.63 | async-start | bytes 1769472
  830.2 302.9 %reduce-scatter.76.cloned.1.call-start = ((), (), s32[]{:S(2)}) async-start(), calls=%async_computation.64 | async-start | bytes 1769472
  837.9 360.1 %reduce-scatter.70.cloned.1.call-start = ((), (), s32[]{:S(2)}) async-start(), calls=%async_computation.61 | async-start | bytes 589824
  843.4 372.0 %all-gather.42.cloned.1.call-start = ((), (), s32[]{:S(2)}) async-start(), calls=%async_computation.40 | async-start | bytes 1310720 | tf_op jit(solution)/shard_map/all_gather | solution.py:303
  844.1 389.4 %all-gather.34.cloned.1.call-start = ((), (), s32[]{:S(2)}) async-start(), calls=%async_computation.28 | async-start | bytes 1310720 | tf_op jit(solution)/shard_map/all_gather | solution.py:300
  844.7 454.8 %reduce-scatter.64.cloned.1.call-start = ((), (), s32[]{:S(2)}) async-start(), calls=%async_computation.50 | async-start | bytes 589824 | tf_op jit(solution)/shard_map/reduce_scatter | solution.py:313
  849.4 515.1 %reduce-scatter.66.cloned.1.call-start = ((), (), s32[]{:S(2)}) async-start(), calls=%async_computation.51 | async-start | bytes 589824 | tf_op jit(solution)/shard_map/reduce_scatter | solution.py:316
  853.9 575.4 %reduce-scatter.68.cloned.1.call-start = ((), (), s32[]{:S(2)}) async-start(), calls=%async_computation.52 | async-start | bytes 589824 | tf_op jit(solution)/shard_map/reduce_scatter | solution.py:319
  859.6 612.8 %all-gather.48.cloned.1.call-start = ((), (), s32[]{:S(2)}) async-start(), calls=%async_computation.49 | async-start | bytes 1310720 | tf_op jit(solution)/shard_map/all_gather | solution.py:303
  897.2 577.5 %all-gather.46.cloned.1.call-start = ((), (), s32[]{:S(2)}) async-start(), calls=%async_computation.46 | async-start | bytes 1310720 | tf_op jit(solution)/shard_map/all_gather | solution.py:303
  930.6 552.6 %all-gather.44.cloned.1.call-start = ((), (), s32[]{:S(2)}) async-start(), calls=%async_computation.43 | async-start | bytes 1310720 | tf_op jit(solution)/shard_map/all_gather | solution.py:303
  931.2 570.3 %all-gather.40.cloned.1.call-start = ((), (), s32[]{:S(2)}) async-start(), calls=%async_computation.37 | async-start | bytes 1310720 | tf_op jit(solution)/shard_map/all_gather | solution.py:300
  932.0 587.9 %all-gather.38.cloned.1.call-start = ((), (), s32[]{:S(2)}) async-start(), calls=%async_computation.34 | async-start | bytes 1310720 | tf_op jit(solution)/shard_map/all_gather | solution.py:300
  932.7 605.4 %all-gather.36.cloned.1.call-start = ((), (), s32[]{:S(2)}) async-start(), calls=%async_computation.31 | async-start | bytes 1310720 | tf_op jit(solution)/shard_map/all_gather | solution.py:300
  (285 other events, 4234.8 us)
Sparse Core Ops, SparseCore 0:
  10.1 19.4 all-gather.49
  31.7 16.6 all-gather.51
  50.6 16.6 all-gather.53
  69.3 16.6 all-gather.55
  87.5 16.6 all-gather.57
  190.8 30.5 reduce-scatter.31
  223.5 42.9 all-gather.31
  268.5 41.1 all-gather.29
  311.8 41.1 all-gather.27
  354.4 14.8 all-gather.59
  371.8 31.1 reduce-scatter.35
  406.0 31.1 reduce-scatter.47
  439.7 31.2 reduce-scatter.51
  472.4 21.3 all-gather.63
  496.7 31.0 reduce-scatter.43
  529.3 16.6 all-gather.61
  548.4 31.1 reduce-scatter.39
  582.0 31.1 reduce-scatter.49
  615.7 31.1 reduce-scatter.53
  649.2 31.1 reduce-scatter.33
  683.5 31.1 reduce-scatter.59
  717.2 31.1 reduce-scatter.55
  757.9 35.1 reduce-scatter.37
  796.1 31.1 reduce-scatter.61
  829.8 31.1 reduce-scatter.57
  863.4 31.1 reduce-scatter.45
  897.0 31.1 reduce-scatter.41
  931.7 65.5 reduce-scatter.71
  1000.7 64.4 reduce-scatter.73
  1068.4 64.5 reduce-scatter.75
  1136.4 61.5 reduce-scatter.69
  1199.6 15.6 all-gather.41
  1216.7 16.6 all-gather.33
  1236.8 62.6 reduce-scatter.63
  1302.8 61.6 reduce-scatter.65
  1367.6 61.6 reduce-scatter.67
  1430.7 16.0 all-gather.47
  1448.4 16.6 all-gather.45
  1466.5 16.6 all-gather.43
  1484.8 16.6 all-gather.39
  1503.1 16.6 all-gather.37
  1521.4 16.6 all-gather.35
